TPU v7x, 32 devices: a whole 2x2x4 slice. The times are simulated.
32 devices in a mesh: row: 4 (over z), col: 2 (over x), dp: 4 (over y, core).
Axes of the slice: x: 2, y: 2, z: 4, core: 2. Of those that a mesh axis runs over, the one named last changes fastest.
Arguments:
- tokens: bfloat16 [1536, 6144], P('dp', 'row'), parts along dimension 0, may hold values from -120 to 120
- norm_gain: float32 [6144], P('row'), may hold values from 0.25 to 1.75
- qkv_weight: bfloat16 [6144, 3, 3072], P('row', None, 'col'), may hold values from -2.5 to 2.5
- out_weight: bfloat16 [3072, 6144], P('col', 'row'), may hold values from -0.109375 to 0.109375
Outputs:
- projected: bfloat16 [1536, 6144], P('dp', 'row'), parts along dimension 0
There are 4 independent parts, one for each index of `dp`. A program takes and returns all parts, laid end to end along the dimension named above; an argument that names none is the same for every part. Nothing has to cross between parts.
All inputs are finite; a program needn't handle non-finite values.
Results may differ from a plain program's by a relative error of at most 0.025.
Values may be sent and summed in bfloat16 or wider, within the bound.
A program may use at most 64 MiB of HBM per device.

v0:
```python
import math
import jax
import jax.numpy as jnp
from jax import lax
from jax.sharding import PartitionSpec as P

K = 128
EPSILON = 1e-05


def attend(queries, key_rows, value_rows):
    query_total = queries.shape[0]
    head_count = queries.shape[1] // K
    scaling = 1.0 / math.sqrt(K)
    split_keys = key_rows.reshape(key_rows.shape[0], head_count, K)
    split_values = value_rows.reshape(value_rows.shape[0], head_count, K)
    split_queries = queries.reshape(query_total, head_count, K)
    scores = (
        jnp.einsum("qhd,khd->hqk", split_queries, split_keys, preferred_element_type=jnp.float32)
        * scaling
    )
    largest = jnp.max(scores, axis=2, keepdims=True)
    exponent = jnp.exp(scores - largest)
    softmax_weights = (exponent / jnp.sum(exponent, axis=2, keepdims=True)).astype(jnp.bfloat16)
    mixed = jnp.einsum(
        "hqk,khd->qhd", softmax_weights, split_values, preferred_element_type=jnp.float32
    )
    result = mixed.astype(jnp.bfloat16)
    return result.reshape(query_total, head_count * K)


def shards(tokens, norm_gain, qkv_weight, out_weight):
    row_count, block_width = tokens.shape
    full_width = block_width * lax.axis_size("row")
    values = tokens.astype(jnp.float32)
    totals, squares = lax.psum(
        (jnp.sum(values, axis=1, keepdims=True), jnp.sum(values * values, axis=1, keepdims=True)),
        "row",
    )
    average = totals / full_width
    variance = squares / full_width - average * average
    centered = values - average
    normed = (centered * lax.rsqrt(variance + EPSILON) * norm_gain).astype(jnp.bfloat16)
    head_columns = qkv_weight.shape[2]
    partial_value = jnp.dot(
        normed,
        qkv_weight.reshape(block_width, 3 * head_columns),
        preferred_element_type=jnp.float32,
    )
    summed = lax.psum(partial_value.astype(jnp.bfloat16), "row").reshape(row_count, 3, head_columns)
    attended = attend(summed[:, 0], summed[:, 1], summed[:, 2])
    partial_out = jnp.dot(attended, out_weight, preferred_element_type=jnp.float32)
    return lax.psum(partial_out.astype(jnp.bfloat16), "col")


def solution(mesh):
    in_specs = (P("dp", "row"), P("row"), P("row", None, "col"), P("col", "row"))
    out_specs = P("dp", "row")
    return jax.shard_map(shards, mesh=mesh, in_specs=in_specs, out_specs=out_specs, check_vma=False)
```

profile of v0, /device:TPU:0, one launch (start us, length us, event | category | flops | bytes accessed | tf_op | source)
XLA Modules:
  0.0 253.6 jit_solution(16139016888201354875)
XLA Ops:
  6.5 0.0 all-reduce.4.cloned.1.call-start
  6.5 1.7 convert_reduce_fusion
  8.3 0.0 copy-start
  8.3 18.6 %copy.7 = bf16[1536,3,1536]{0,2,1:T(8,128)(2,1)} copy(bf16[1536,3,1536]{2,0,1:T(8,128)(2,1)} %param.6) | data formatting | bytes 28311552 | tf_op args[2]
  26.9 13.5 %all-reduce = (f32[384,1]{0,1:T(1,128)S(1)}, f32[384,1]{0,1:T(1,128)S(1)}) all-reduce(f32[384,1]{0,1:T(1,128)S(1)} %broadcast_in_dim.4, f32[384,1]{0,1:T(1,128)S(1)} %broadcast_in_dim.10), channel_id=1, replica_groups=mesh['row'=4,'col'=2,'dp'=4] {'row'}, use_global_device_ids=true, to_apply=%region_1.0 | all-reduce | flops 768 | bytes 6144 | tf_op jit(solution)/shard_map/psum | solution.py:36
  40.4 0.0 copy-done
  40.4 9.4 %convolution_convert_fusion = bf16[384,4608]{1,0:T(8,128)(2,1)S(1)} fusion(bf16[1536,4608]{0,1:T(8,128)(2,1)} %bitcast.16, bf16[384,1536]{1,0:T(8,128)(2,1)} %param.4, f32[1536]{0:T(1024)S(1)} %copy-done, f32[384]{0:T(512)S(1)} %get-tuple-element.8, f32[384]{0:T(512)S(1)} %get-tuple-element.7), kind=kOutput, calls=%fused_computation.3 | convolution fusion | flops 5440536576 | bytes 18883584 | tf_op jit(solution)/shard_map/dot_general | solution.py:45
  49.9 3.6 %copy.8 = bf16[384,4608]{0,1:T(8,128)(2,1)} copy(bf16[384,4608]{1,0:T(8,128)(2,1)S(1)} %convolution_convert_fusion) | data formatting | bytes 7077888 | tf_op jit(solution)/shard_map/convert_element_type | solution.py:50
  53.5 0.0 all-reduce.4.cloned.1.call-update
  53.5 0.0 all-reduce.6.cloned.1.call-start
  53.6 132.1 %all-reduce.4.cloned.1.call-done = bf16[384,3,1536]{0,2,1:T(8,128)(2,1)} async-done(((bf16[384,3,1536]{0,2,1:T(8,128)(2,1)}), bf16[384,3,1536]{0,2,1:T(8,128)(2,1)}) %all-reduce.4.cloned.1.call-update) | async-done | bytes 3538960 | tf_op jit(solution)/shard_map/psum | solution.py:50
  185.7 2.3 fusion.18
  188.0 4.9 %fusion.19 = (f32[12,384]{1,0:T(8,128)}, f32[12,384,384]{1,2,0:T(8,128)}) fusion(bf16[384,12,128]{0,2,1:T(8,128)(2,1)S(1)} %bitcast.20, bf16[384,12,128]{0,2,1:T(8,128)(2,1)S(1)} %bitcast.19), kind=kOutput, calls=%fused_computation.25 | convolution fusion | flops 458293632 | bytes 9455616 | tf_op jit(solution)/shard_map/sub | solution.py:23
  192.9 4.0 %fusion.10 = bf16[12,128,384]{2,1,0:T(8,128)(2,1)S(1)} fusion(bf16[384,12,128]{0,2,1:T(8,128)(2,1)S(1)} %bitcast.18, f32[12,384,384]{1,2,0:T(8,128)} %get-tuple-element.15, f32[12,384]{1,0:T(8,128)} %get-tuple-element.14), kind=kOutput, calls=%fused_computation.16 | convolution fusion | flops 457113600 | bytes 9455616 | tf_op jit(solution)/shard_map/hqk,khd->qhd/dot_general | solution.py:25
  196.9 5.4 %convolution_convert_fusion.1 = bf16[384,1536]{1,0:T(8,128)(2,1)} fusion(bf16[384,1536]{0,1:T(8,128)(2,1)S(1)} %bitcast.21, bf16[1536,1536]{1,0:T(8,128)(2,1)} %param.7), kind=kOutput, calls=%fused_computation.11 | convolution fusion | flops 1812529152 | bytes 7077888 | tf_op jit(solution)/shard_map/dot_general | solution.py:52
  202.3 0.0 all-reduce.6.cloned.1.call-update
  202.3 42.1 %all-reduce.6.cloned.1.call-done = bf16[384,1536]{1,0:T(8,128)(2,1)} async-done(((bf16[384,1536]{1,0:T(8,128)(2,1)}), bf16[384,1536]{1,0:T(8,128)(2,1)}) %all-reduce.6.cloned.1.call-update) | async-done | bytes 1179664 | tf_op jit(solution)/shard_map/psum | solution.py:53
  244.4 2.4 copy.17
  (3 shorter events, 0.0 us)
Async XLA Ops:
  6.5 179.1 %all-reduce.4.cloned.1.call-start = ((), (), s32[]{:S(2)}) async-start(), calls=%async_computation | async-start | bytes 7077888 | tf_op jit(solution)/shard_map/psum | solution.py:50
  8.3 32.1 %copy-start = (f32[1536]{0:T(1024)S(1)}, f32[1536]{0:T(1024)}, u32[]{:S(2)}) copy-start(f32[1536]{0:T(1024)} %param.5) | copy-start | bytes 18436
  53.5 190.9 %all-reduce.6.cloned.1.call-start = ((), (), s32[]{:S(2)}) async-start(), calls=%async_computation.1 | async-start | bytes 2359296 | tf_op jit(solution)/shard_map/psum | solution.py:53
Sparse Core Ops, SparseCore 0:
  53.6 131.9 all-reduce.3
  202.4 41.9 all-reduce.5
where the time goes:
time: 254 us
  waiting for transfers between devices  174 us (69%)
  local copies, waits for them, and re-layouts  27 us (11%)
  matrix products  23.7 us (9%)
  blocking collectives  13.5 us (5%)
  between operations  13.4 us (5%)
    psum x1, waiting for transfers between devices, shards(): lax.psum(partial_value.astype(jnp.bfloat16), 'row')  132 us
    psum x1, waiting for transfers between devices, shards(): return lax.psum(partial_out.astype(jnp.bfloat16), 'col')  42.1 us
    unnamed x4, local copies, waits for them, and re-layouts  21 us
    psum x1, blocking collectives, shards(): lax.psum((jnp.sum(values, axis=1, keepdims=True), jnp.sum(values * values...  13.5 us
    dot_general x1, matrix products, shards(): jnp.dot(normed, qkv_weight.reshape(block_width, 3 * head_columns), prefer...  9.45 us
    dot_general x1, matrix products, shards(): jnp.dot(attended, out_weight, preferred_element_type=jnp.float32)  5.37 us
  transfers between devices with their start and end apart: 2, of which 2 were waited for; matrix products, arithmetic and copies ran while one was open for 0% of the time, Pallas kernels for 0%

commit v1 on v0

--- a/solution.py
+++ b/solution.py
@@ -50,7 +50,7 @@
     summed = lax.psum(partial_value.astype(jnp.bfloat16), "row").reshape(row_count, 3, head_columns)
     attended = attend(summed[:, 0], summed[:, 1], summed[:, 2])
     partial_out = jnp.dot(attended, out_weight, preferred_element_type=jnp.float32)
-    return lax.psum(partial_out.astype(jnp.bfloat16), "col")
+    return jnp.sum(lax.all_gather(partial_out.astype(jnp.bfloat16), "col"), axis=0)
 
 
 def solution(mesh):

time: 254 us -> 248 us (0.976)
  waiting for transfers between devices: 174 us -> 167 us
  other arithmetic: 1.76 us -> 5.19 us
    psum x1 -> x0, waiting for transfers between devices: 42.1 us -> none  [shards(): return lax.psum(partial_out.astype(jnp.bfloat16), 'col')]
    all_gather x0 -> x1, waiting for transfers between devices: none -> 35.2 us  [shards(): lax.all_gather(partial_out.astype(jnp.bfloat16), 'col')]
    reduce_sum x0 -> x1, other arithmetic: none -> 3.43 us  [shards(): jnp.sum(lax.all_gather(partial_out.astype(jnp.bfloat16), 'col'), axis=0)]
    unnamed x4 -> x3, local copies, waits for them, and re-layouts: 21 us -> 18.7 us
where the time goes in v1:
time: 248 us
  waiting for transfers between devices  167 us (67%)
  local copies, waits for them, and re-layouts  24.6 us (10%)
  matrix products  23.7 us (10%)
  blocking collectives  13.5 us (5%)
  between operations  13.4 us (5%)
  other arithmetic  5.19 us (2%)
    psum x1, waiting for transfers between devices, shards(): lax.psum(partial_value.astype(jnp.bfloat16), 'row')  132 us
    all_gather x1, waiting for transfers between devices, shards(): lax.all_gather(partial_out.astype(jnp.bfloat16), 'col')  35.2 us
    unnamed x3, local copies, waits for them, and re-layouts  18.7 us
    psum x1, blocking collectives, shards(): lax.psum((jnp.sum(values, axis=1, keepdims=True), jnp.sum(values * values...  13.5 us
    dot_general x1, matrix products, shards(): jnp.dot(normed, qkv_weight.reshape(block_width, 3 * head_columns), prefer...  9.45 us
    dot_general x1, matrix products, shards(): jnp.dot(attended, out_weight, preferred_element_type=jnp.float32)  5.37 us
  transfers between devices with their start and end apart: 2, of which 2 were waited for; matrix products, arithmetic and copies ran while one was open for 0% of the time, Pallas kernels for 0%

profile of v1, /device:TPU:0, one launch (start us, length us, event | category | flops | bytes accessed | tf_op | source)
XLA Modules:
  0.0 247.7 jit_solution(9701323430951590879)
XLA Ops:
  6.5 0.0 all-reduce.3.cloned.1.call-start
  6.5 1.7 convert_reduce_fusion
  8.3 0.0 copy-start
  8.3 18.6 %copy.7 = bf16[1536,3,1536]{0,2,1:T(8,128)(2,1)} copy(bf16[1536,3,1536]{2,0,1:T(8,128)(2,1)} %param.6) | data formatting | bytes 28311552 | tf_op args[2]
  26.9 13.5 %all-reduce = (f32[384,1]{0,1:T(1,128)S(1)}, f32[384,1]{0,1:T(1,128)S(1)}) all-reduce(f32[384,1]{0,1:T(1,128)S(1)} %broadcast_in_dim.4, f32[384,1]{0,1:T(1,128)S(1)} %broadcast_in_dim.10), channel_id=1, replica_groups=mesh['row'=4,'col'=2,'dp'=4] {'row'}, use_global_device_ids=true, to_apply=%region_1.0 | all-reduce | flops 768 | bytes 6144 | tf_op jit(solution)/shard_map/psum | solution.py:36
  40.4 0.0 copy-done
  40.4 9.4 %convolution_convert_fusion = bf16[384,4608]{1,0:T(8,128)(2,1)S(1)} fusion(bf16[1536,4608]{0,1:T(8,128)(2,1)} %bitcast.17, bf16[384,1536]{1,0:T(8,128)(2,1)} %param.4, f32[1536]{0:T(1024)S(1)} %copy-done, f32[384]{0:T(512)S(1)} %get-tuple-element.8, f32[384]{0:T(512)S(1)} %get-tuple-element.7), kind=kOutput, calls=%fused_computation.3 | convolution fusion | flops 5440536576 | bytes 18883584 | tf_op jit(solution)/shard_map/dot_general | solution.py:45
  49.9 3.6 %copy.8 = bf16[384,4608]{0,1:T(8,128)(2,1)} copy(bf16[384,4608]{1,0:T(8,128)(2,1)S(1)} %convolution_convert_fusion) | data formatting | bytes 7077888 | tf_op jit(solution)/shard_map/convert_element_type | solution.py:50
  53.5 0.0 all-reduce.3.cloned.1.call-update
  53.5 0.0 all-gather.3.cloned.1.call-start
  53.6 132.1 %all-reduce.3.cloned.1.call-done = bf16[384,3,1536]{0,2,1:T(8,128)(2,1)} async-done(((bf16[384,3,1536]{0,2,1:T(8,128)(2,1)}), bf16[384,3,1536]{0,2,1:T(8,128)(2,1)}) %all-reduce.3.cloned.1.call-update) | async-done | bytes 3538960 | tf_op jit(solution)/shard_map/psum | solution.py:50
  185.7 2.3 fusion.18
  188.0 4.9 %fusion.19 = (f32[12,384]{1,0:T(8,128)}, f32[12,384,384]{1,2,0:T(8,128)}) fusion(bf16[384,12,128]{0,2,1:T(8,128)(2,1)S(1)} %bitcast.22, bf16[384,12,128]{0,2,1:T(8,128)(2,1)S(1)} %bitcast.21), kind=kOutput, calls=%fused_computation.25 | convolution fusion | flops 458293632 | bytes 9455616 | tf_op jit(solution)/shard_map/sub | solution.py:23
  192.9 4.0 %fusion.10 = bf16[12,128,384]{2,1,0:T(8,128)(2,1)S(1)} fusion(bf16[384,12,128]{0,2,1:T(8,128)(2,1)S(1)} %bitcast.20, f32[12,384,384]{1,2,0:T(8,128)} %get-tuple-element.15, f32[12,384]{1,0:T(8,128)} %get-tuple-element.14), kind=kOutput, calls=%fused_computation.16 | convolution fusion | flops 457113600 | bytes 9455616 | tf_op jit(solution)/shard_map/hqk,khd->qhd/dot_general | solution.py:25
  196.9 5.4 %convolution_convert_fusion.1 = bf16[384,1536]{1,0:T(8,128)(2,1)} fusion(bf16[384,1536]{0,1:T(8,128)(2,1)S(1)} %bitcast.23, bf16[1536,1536]{1,0:T(8,128)(2,1)} %param.7), kind=kOutput, calls=%fused_computation.11 | convolution fusion | flops 1812529152 | bytes 7077888 | tf_op jit(solution)/shard_map/dot_general | solution.py:52
  202.3 0.0 all-gather.3.cloned.1.call-update
  202.3 35.2 %all-gather.3.cloned.1.call-done = bf16[768,1536]{1,0:T(8,128)(2,1)} async-done(((bf16[384,1536]{1,0:T(8,128)(2,1)}), bf16[768,1536]{1,0:T(8,128)(2,1)}) %all-gather.3.cloned.1.call-update) | async-done | bytes 2359312 | tf_op jit(solution)/shard_map/all_gather | solution.py:53
  237.5 3.4 %reduce_sum.42 = bf16[384,1536]{1,0:T(8,128)(2,1)} reduce(bf16[2,384,1536]{2,1,0:T(8,128)(2,1)} %bitcast.19, bf16[]{:T(256)} %constant.13.clone.1), dimensions={0}, to_apply=%region_7.0 | reduce | flops 589824 | bytes 3538946 | tf_op jit(solution)/shard_map/reduce_sum | solution.py:53
  (3 shorter events, 0.0 us)
Async XLA Ops:
  6.5 179.1 %all-reduce.3.cloned.1.call-start = ((), (), s32[]{:S(2)}) async-start(), calls=%async_computation | async-start | bytes 7077888 | tf_op jit(solution)/shard_map/psum | solution.py:50
  8.3 32.1 %copy-start = (f32[1536]{0:T(1024)S(1)}, f32[1536]{0:T(1024)}, u32[]{:S(2)}) copy-start(f32[1536]{0:T(1024)} %param.5) | copy-start | bytes 18436
  53.5 183.9 %all-gather.3.cloned.1.call-start = ((), (), s32[]{:S(2)}) async-start(), calls=%async_computation.1 | async-start | bytes 3538944 | tf_op jit(solution)/shard_map/all_gather | solution.py:53
Sparse Core Ops, SparseCore 0:
  53.6 131.9 all-reduce.2
  202.4 35.0 all-gather.2
